TPU v7x, 32 devices: a whole 2x2x4 slice. The times are simulated.
32 devices in a mesh: cp: 4 (over z), tp: 8 (over y, x, core).
Axes of the slice: x: 2, y: 2, z: 4, core: 2. Of those that a mesh axis runs over, the one named last changes fastest.
Arguments:
- checkpoint: bfloat16 [2048, 8192], P('cp', 'tp'), may hold values from -6 to 6
- norm_gain: float32 [8192], replicated, may hold values from 0.1 to 1.9
- query_weight: bfloat16 [8192, 8192], P(None, 'tp'), may hold values from -4 to 4
- key_weight: bfloat16 [8192, 1024], P(None, 'tp'), may hold values from -1 to 1
- value_weight: bfloat16 [8192, 1024], P(None, 'tp'), may hold values from -0.0625 to 0.0625
- output_weight: bfloat16 [8192, 8192], P('tp'), may hold values from -0.09375 to 0.09375
- block_order: int32 [8], replicated, may hold values from 0 to 7, each once
Outputs:
- projected: bfloat16 [2048, 8192], P('cp', 'tp')
- log_normalizer: float32 [64, 2048], P('tp', 'cp')
Inputs may be any that keep to these rules, and one draw needn't show every extreme that they name: `block_order`: each of 0 to 7 once.
All inputs are finite; a program needn't handle non-finite values.
Results may differ from a plain program's by a relative error of at most 0.019.
Values may be sent and summed in bfloat16 or wider, within the bound.
No kernel may reach another device: no remote copies, remote signals or barrier semaphores. Data moves between devices by JAX's collectives and lax.ppermute only.
A program may use at most 128 MiB of HBM per device.

v0:
```python
import math
import jax
import jax.numpy as jnp
from jax import lax
from jax.sharding import PartitionSpec as P

KV_HEADS = 8
HEAD_DIM = 128
rope_base = 500000.0
norm_epsilon = 1e-05
masked_score = -1e30


def partner_2(block, axis, stride):
    count = lax.axis_size(axis)
    route = []
    for low in range(count):
        high = low | 1 << stride
        if high != low and high < count:
            route += [(low, high), (high, low)]
    return lax.ppermute(block, axis, route)


def from_behind(block, axis, distance):
    devices = range(lax.axis_size(axis))
    route = [((i - distance) % len(devices), i) for i in devices]
    return lax.ppermute(block, axis, route)


def turn_pairs(matrix, positions, first_pair):
    pair_count = matrix.shape[-1] // 2
    pair_index = (first_pair + jnp.arange(pair_count, dtype=jnp.int32)).astype(jnp.float32)
    inverse_rates = rope_base ** (-2.0 * pair_index / HEAD_DIM)
    angles = positions.astype(jnp.float32)[:, None] * inverse_rates[None, :]
    cosine = jnp.cos(angles)[:, None, :]
    sine_part = jnp.sin(angles)[:, None, :]
    paired = matrix.reshape(matrix.shape[0], matrix.shape[1], pair_count, 2)
    former = paired[..., 0]
    latter = paired[..., 1]
    turned = jnp.stack(
        [former * cosine - latter * sine_part, former * sine_part + latter * cosine], axis=-1
    )
    return turned.reshape(matrix.shape)


def shards(
    checkpoint, norm_gain, query_weight, key_weight, value_weight, output_weight, block_order
):
    tok_rows = checkpoint.shape[0]
    block_rows = tok_rows // 2
    local_heads = query_weight.shape[1] // HEAD_DIM
    key_columns = key_weight.shape[1]
    context_rank = lax.axis_index("cp")
    tensor_rank = lax.axis_index("tp")
    row_offsets = jnp.arange(block_rows, dtype=jnp.int32)
    own_blocks = lax.dynamic_slice_in_dim(block_order, 2 * context_rank, 2)
    own_positions = (own_blocks[:, None] * block_rows + row_offsets[None, :]).reshape(tok_rows)
    gathered = lax.all_gather(checkpoint, "tp", axis=1, tiled=True)
    widened = gathered.astype(jnp.float32)
    mean_square = jnp.mean(widened * widened, axis=-1, keepdims=True)
    normed = (widened * lax.rsqrt(mean_square + norm_epsilon) * norm_gain).astype(jnp.bfloat16)
    query_features = jnp.dot(normed, query_weight, preferred_element_type=jnp.float32)
    key_features = jnp.dot(normed, key_weight, preferred_element_type=jnp.float32)
    value_features = jnp.dot(normed, value_weight, preferred_element_type=jnp.float32)
    queries = turn_pairs(
        query_features.reshape(tok_rows, local_heads, HEAD_DIM), own_positions, 0
    ).astype(jnp.bfloat16)
    sharing = lax.axis_size("tp") // KV_HEADS
    part_of_head = tensor_rank % sharing
    key_part = turn_pairs(
        key_features.reshape(tok_rows, 1, key_columns),
        own_positions,
        part_of_head * (key_columns // 2),
    )
    key_part = key_part.astype(jnp.bfloat16).reshape(tok_rows, key_columns)
    value_part = value_features.astype(jnp.bfloat16)
    own_pair = jnp.stack([key_part, value_part])
    if sharing == 2:
        partner = partner_2(own_pair, "tp", 0)
        lower_first = jnp.concatenate([own_pair, partner], axis=-1)
        upper_first = jnp.concatenate([partner, own_pair], axis=-1)
        key_value = jnp.where(part_of_head == 0, lower_first, upper_first)
    else:
        key_value = own_pair
    score_scale = 1.0 / math.sqrt(HEAD_DIM)

    def absorb(running, query_slot, key_block, key_rows, value_rows):
        query_block = own_blocks[query_slot]
        top_scores, totals, weighted = running
        query_rows = queries[query_slot * block_rows : (query_slot + 1) * block_rows]
        scores = (
            jnp.einsum("qhd,kd->qhk", query_rows, key_rows, preferred_element_type=jnp.float32)
            * score_scale
        )
        query_places = query_block * block_rows + row_offsets
        key_places = key_block * block_rows + row_offsets
        allowed = (key_places[None, :] <= query_places[:, None])[:, None, :]
        scores = jnp.where(allowed, scores, masked_score)
        old_top = top_scores[query_slot]
        new_top = jnp.maximum(old_top, jnp.max(scores, axis=-1))
        weights = jnp.where(allowed, jnp.exp(scores - new_top[..., None]), 0.0)
        shrink = jnp.exp(old_top - new_top)
        new_total = totals[query_slot] * shrink + jnp.sum(weights, axis=-1)
        new_sum = weighted[query_slot] * shrink[..., None] + jnp.einsum(
            "qhk,kd->qhd",
            weights.astype(jnp.bfloat16),
            value_rows,
            preferred_element_type=jnp.float32,
        )
        return (
            top_scores.at[query_slot].set(new_top),
            totals.at[query_slot].set(new_total),
            weighted.at[query_slot].set(new_sum),
        )

    def visit_rows(running, key_value_rows, first_row):
        block_count = key_value_rows.shape[1] // block_rows

        def one_block(block_index, current):
            rows_here = lax.dynamic_slice_in_dim(
                key_value_rows, block_index * block_rows, block_rows, 1
            )
            stored = first_row // block_rows + block_index
            key_block = lax.dynamic_index_in_dim(block_order, stored, 0, keepdims=False)
            for query_slot in range(2):
                current = absorb(current, query_slot, key_block, rows_here[0], rows_here[1])
            return current

        return lax.fori_loop(0, block_count, one_block, running)

    running = (
        jnp.full((2, block_rows, local_heads), masked_score, jnp.float32),
        jnp.zeros((2, block_rows, local_heads), jnp.float32),
        jnp.zeros((2, block_rows, local_heads, HEAD_DIM), jnp.float32),
    )
    running = visit_rows(running, key_value, context_rank * tok_rows)
    context_size = lax.axis_size("cp")

    def pass_turn(turn_index, carried):
        current, travelling = carried
        travelling = from_behind(travelling, "cp", 1)
        source = (context_rank - turn_index) % context_size
        return (visit_rows(current, travelling, source * tok_rows), travelling)

    running, unused = lax.fori_loop(1, context_size, pass_turn, (running, key_value))
    top_scores, totals, weighted = running
    attended = (
        (weighted / totals[..., None])
        .astype(jnp.bfloat16)
        .reshape(tok_rows, local_heads * HEAD_DIM)
    )
    normalizer = jnp.transpose((top_scores + jnp.log(totals)).reshape(tok_rows, local_heads))
    partial_terms = jnp.dot(attended, output_weight, preferred_element_type=jnp.float32)
    projected = lax.psum_scatter(
        partial_terms.astype(jnp.bfloat16), "tp", scatter_dimension=1, tiled=True
    )
    return (projected, normalizer)


def solution(mesh):
    return jax.shard_map(
        shards,
        mesh=mesh,
        in_specs=(
            P("cp", "tp"),
            P(),
            P(None, "tp"),
            P(None, "tp"),
            P(None, "tp"),
            P("tp", None),
            P(),
        ),
        out_specs=(P("cp", "tp"), P("tp", "cp")),
        check_vma=False,
    )
```

profile of v0, /device:TPU:0, one launch (start us, length us, event | category | flops | bytes accessed | tf_op | source)
XLA Modules:
  0.0 284.2 jit_solution(17932145199853954866)
XLA Ops:
  7.2 0.7 all-gather.2.cloned.1.call-update
  8.0 0.7 broadcast_multiply_fusion
  11.1 55.8 %all-gather.2.cloned.1.call-done = bf16[512,8192]{1,0:T(8,128)(2,1)} async-done(((bf16[512,1024]{1,0:T(8,128)(2,1)}), bf16[512,8192]{1,0:T(8,128)(2,1)}) %all-gather.2.cloned.1.call-update) | async-done | bytes 8388624 | tf_op jit(solution)/shard_map/all_gather | solution.py:58
  66.9 5.1 %fusion.92 = f32[512]{0:T(512)S(1)} fusion(bf16[512,8192]{1,0:T(8,128)(2,1)} %all-gather.2.cloned.1.call-done), kind=kLoop, calls=%fused_computation.134 | loop fusion | flops 12582400 | bytes 8390656 | tf_op jit(solution)/shard_map/reduce_sum | solution.py:60
  72.0 15.5 %fusion.106 = f32[512,1024]{0,1:T(8,128)} fusion(bf16[8192,1024]{1,0:T(8,128)(2,1)} %param.39, bf16[512,8192]{1,0:T(8,128)(2,1)} %all-gather.2.cloned.1.call-done, f32[8192]{0:T(1024)S(1)} %copy-done.5, f32[512]{0:T(512)S(1)} %add_rsqrt_fusion), kind=kOutput, calls=%fused_computation.165 | convolution fusion | flops 8606711808 | bytes 27297792 | tf_op jit(solution)/shard_map/dot_general | solution.py:62
  87.6 3.5 %reshape_reshape.7 = f32[512,8,64,2]{0,3,2,1:T(2,128)} reshape(f32[512,1024]{0,1:T(8,128)} %fusion.106) | data formatting | bytes 4194304 | tf_op jit(solution)/shard_map/reshape;reshape | solution.py:37
  91.0 5.8 %fusion.109 = f32[512,128]{0,1:T(8,128)S(1)} fusion(bf16[8192,128]{1,0:T(8,128)(2,1)S(1)} %copy-done, bf16[512,8192]{1,0:T(8,128)(2,1)} %all-gather.2.cloned.1.call-done, f32[8192]{0:T(1024)S(1)} %copy-done.5, f32[512]{0:T(512)S(1)} %add_rsqrt_fusion), kind=kOutput, calls=%fused_computation.166 | convolution fusion | flops 1090519040 | bytes 10782720 | tf_op jit(solution)/shard_map/dot_general | solution.py:63
  98.4 2.9 %subtract_convert_fusion = (bf16[512,8,64,1]{0,3,2,1:T(2,128)(2,1)S(1)}, bf16[512,8,64,1]{0,3,2,1:T(2,128)(2,1)S(1)}) fusion(f32[512,8,64,2]{0,3,2,1:T(2,128)S(1)} %copy-done.2, f32[512,64]{0,1:T(8,128)S(1)} %get-tuple-element.1680, f32[512,64]{0,1:T(8,128)S(1)} %get-tuple-element.1679), kind=kLoop, calls=%fused_computation.145 | loop fusion | flops 2097152 | bytes 3407872 | tf_op jit(solution)/shard_map/convert
  101.3 2.2 pad_maximum_fusion
  103.5 1.1 copy.45
  104.7 1.2 copy.46
  105.9 6.4 %fusion.95 = bf16[1,512,128]{2,1,0:T(8,128)(2,1)S(1)} fusion(bf16[8192,128]{1,0:T(8,128)(2,1)} %param.41, bf16[512,8192]{1,0:T(8,128)(2,1)} %all-gather.2.cloned.1.call-done, f32[8192]{0:T(1024)S(1)} %copy-done.5, f32[512]{0:T(512)S(1)} %add_rsqrt_fusion), kind=kOutput, calls=%fused_computation.140 | convolution fusion | flops 1090584576 | bytes 10651648 | tf_op jit(solution)/shard_map/dot_general | solution.py:64
  112.3 0.7 pad_maximum_fusion.1
  113.2 11.7 %while.100 = (s32[]{:T(128)}, f32[2,256,8]{1,2,0:T(8,128)S(1)}, f32[2,256,8]{1,2,0:T(8,128)S(1)}, f32[2,256,8,128]{3,1,2,0:T(8,128)S(1)}, s32[]{:T(128)}, /*inde...) while((s32[]{:T(128)}, f32[2,256,8]{1,2,0:T(8,128)S(1)}, ...), condition=%wide.region_6.7_spmd.clone.clone, body=%wide.region_1.6_spmd.clone.clone.sunk | while | flops 551699200 | bytes 24107364 | solution.py:129
  113.2 0.7 dynamic_slice.54
  115.9 0.9 fusion.153
  118.1 0.9 fusion.155
  119.1 0.7 dynamic_slice.54
  121.7 0.9 fusion.153
  124.0 0.9 fusion.155
  124.9 65.2 %while.102 = (s32[]{:T(128)}, f32[2,256,8]{1,2,0:T(8,128)S(1)}, f32[2,256,8]{1,2,0:T(8,128)S(1)}, f32[2,256,8,128]{3,1,2,0:T(8,128)S(1)}, bf16[2,512,128]{2,1,0:...) while((s32[]{:T(128)}, f32[2,256,8]{1,2,0:T(8,128)S(1)}, ...), condition=%wide.region_14.15_spmd.clone.clone, body=%wide.region_7.14_spmd.clone.clone.sunk | while | flops 551699200 | bytes 24634376 | solution.py:145
  124.9 1.5 collective-permute-start
  126.5 9.0 %collective-permute-done = bf16[2,512,128]{2,1,0:T(8,128)(2,1)S(1)} collective-permute-done((bf16[2,512,128]{2,1,0:T(8,128)(2,1)}, bf16[2,512,128]{2,1,0:T(8,128)(2,1)S(1)}, u32[]{:S(2)}, u32[]{:S(2)}) %collective-permute-start) | collective-permute-done | bytes 262176 | tf_op jit(solution)/shard_map/while/body/eval_jaxpr/ppermute | solution.py:27
  135.5 11.4 %while.103 = (s32[]{:T(128)}, f32[2,256,8]{1,2,0:T(8,128)S(1)}, f32[2,256,8]{1,2,0:T(8,128)S(1)}, f32[2,256,8,128]{3,1,2,0:T(8,128)S(1)}, s32[]{:T(128)}, /*inde...) while((s32[]{:T(128)}, f32[2,256,8]{1,2,0:T(8,128)S(1)}, ...), condition=%wide.region_13.13_spmd.clone, body=%wide.region_8.12_spmd.clone.sunk | while | flops 551699200 | bytes 23059792 | solution.py:129
  137.9 0.9 fusion.166
  140.2 0.9 fusion.168
  143.7 0.9 fusion.166
  145.9 0.9 fusion.168
  146.9 0.7 copy.116
  147.6 9.6 %collective-permute-done = bf16[2,512,128]{2,1,0:T(8,128)(2,1)S(1)} collective-permute-done((bf16[2,512,128]{2,1,0:T(8,128)(2,1)}, bf16[2,512,128]{2,1,0:T(8,128)(2,1)S(1)}, u32[]{:S(2)}, u32[]{:S(2)}) %collective-permute-start) | collective-permute-done | bytes 262176 | tf_op jit(solution)/shard_map/while/body/eval_jaxpr/ppermute | solution.py:27
  157.2 11.4 %while.103 = (s32[]{:T(128)}, f32[2,256,8]{1,2,0:T(8,128)S(1)}, f32[2,256,8]{1,2,0:T(8,128)S(1)}, f32[2,256,8,128]{3,1,2,0:T(8,128)S(1)}, s32[]{:T(128)}, /*inde...) while((s32[]{:T(128)}, f32[2,256,8]{1,2,0:T(8,128)S(1)}, ...), condition=%wide.region_13.13_spmd.clone, body=%wide.region_8.12_spmd.clone.sunk | while | flops 551699200 | bytes 23059792 | solution.py:129
  159.7 0.9 fusion.166
  161.9 0.9 fusion.168
  165.4 0.9 fusion.166
  167.7 0.9 fusion.168
  168.6 0.7 copy.116
  169.3 8.7 %collective-permute-done = bf16[2,512,128]{2,1,0:T(8,128)(2,1)S(1)} collective-permute-done((bf16[2,512,128]{2,1,0:T(8,128)(2,1)}, bf16[2,512,128]{2,1,0:T(8,128)(2,1)S(1)}, u32[]{:S(2)}, u32[]{:S(2)}) %collective-permute-start) | collective-permute-done | bytes 262176 | tf_op jit(solution)/shard_map/while/body/eval_jaxpr/ppermute | solution.py:27
  178.0 11.4 %while.103 = (s32[]{:T(128)}, f32[2,256,8]{1,2,0:T(8,128)S(1)}, f32[2,256,8]{1,2,0:T(8,128)S(1)}, f32[2,256,8,128]{3,1,2,0:T(8,128)S(1)}, s32[]{:T(128)}, /*inde...) while((s32[]{:T(128)}, f32[2,256,8]{1,2,0:T(8,128)S(1)}, ...), condition=%wide.region_13.13_spmd.clone, body=%wide.region_8.12_spmd.clone.sunk | while | flops 551699200 | bytes 23059792 | solution.py:129
  180.5 0.9 fusion.166
  182.8 0.9 fusion.168
  186.2 0.9 fusion.166
  188.5 0.9 fusion.168
  189.4 0.7 copy.116
  190.2 1.0 divide_convert_fusion
  191.1 0.7 copy.48
  191.8 16.8 %convolution_convert_fusion = bf16[512,8192]{1,0:T(8,128)(2,1)} fusion(bf16[1024,8192]{1,0:T(8,128)(2,1)} %param.42, bf16[64,8,8,128]{3,2,1,0:T(8,128)(2,1)S(1)} %bitcast.277), kind=kOutput, calls=%fused_computation.137 | convolution fusion | flops 8594128896 | bytes 26214400 | tf_op jit(solution)/shard_map/dot_general | solution.py:153
  208.7 0.6 log_add_fusion
  209.3 68.1 %reduce-scatter.2.cloned.1.call-done = bf16[512,1024]{1,0:T(8,128)(2,1)} async-done(((bf16[512,8192]{1,0:T(8,128)(2,1)}), bf16[512,1024]{1,0:T(8,128)(2,1)}) %reduce-scatter.2.cloned.1.call-update) | async-done | bytes 1048592 | tf_op jit(solution)/shard_map/reduce_scatter | solution.py:154
  (142 shorter events, 27.1 us)
Async XLA Ops:
  7.2 83.9 %copy-start = (bf16[8192,128]{1,0:T(8,128)(2,1)S(1)}, bf16[8192,128]{1,0:T(8,128)(2,1)}, u32[]{:S(2)}) copy-start(bf16[8192,128]{1,0:T(8,128)(2,1)} %param.40) | copy-start | bytes 6291460
  7.2 59.7 %all-gather.2.cloned.1.call-start = ((), (), s32[]{:S(2)}) async-start(), calls=%async_computation.1 | async-start | bytes 9437184 | tf_op jit(solution)/shard_map/all_gather | solution.py:58
  7.9 269.5 %reduce-scatter.2.cloned.1.call-start = ((), (), s32[]{:S(2)}) async-start(), calls=%async_computation.2 | async-start | bytes 9437184 | tf_op jit(solution)/shard_map/reduce_scatter | solution.py:154
  11.1 60.9 %copy-start.5 = (f32[8192]{0:T(1024)S(1)}, f32[8192]{0:T(1024)}, u32[]{:S(2)}) copy-start(f32[8192]{0:T(1024)} %param.38) | copy-start | bytes 98308
  96.8 1.6 copy-start.2
  112.2 0.9 copy-start.4
  113.2 1.6 copy-start.3
  119.1 1.6 copy-start.3
  124.9 10.5 %collective-permute-start = (bf16[2,512,128]{2,1,0:T(8,128)(2,1)}, bf16[2,512,128]{2,1,0:T(8,128)(2,1)S(1)}, u32[]{:S(2)}, u32[]{:S(2)}) collective-permute-start(bf16[2,512,128]{2,1,0:T(8,128)(2,1)} %get-tuple-element.2101), channel_id=1, source_target_pairs={{24,0},{0,8},{8,16},{16,24},{25,1},{1,9},{9,17},{17,25},{26,2},{2,... | collective-permute-start | bytes 786440 | tf_op jit(solution)/shard_map/while/body/eval_jaxpr/ppermute | solution.py:27
  147.6 9.6 %collective-permute-start = (bf16[2,512,128]{2,1,0:T(8,128)(2,1)}, bf16[2,512,128]{2,1,0:T(8,128)(2,1)S(1)}, u32[]{:S(2)}, u32[]{:S(2)}) collective-permute-start(bf16[2,512,128]{2,1,0:T(8,128)(2,1)} %get-tuple-element.2101), channel_id=1, source_target_pairs={{24,0},{0,8},{8,16},{16,24},{25,1},{1,9},{9,17},{17,25},{26,2},{2,... | collective-permute-start | bytes 786440 | tf_op jit(solution)/shard_map/while/body/eval_jaxpr/ppermute | solution.py:27
  169.3 8.7 %collective-permute-start = (bf16[2,512,128]{2,1,0:T(8,128)(2,1)}, bf16[2,512,128]{2,1,0:T(8,128)(2,1)S(1)}, u32[]{:S(2)}, u32[]{:S(2)}) collective-permute-start(bf16[2,512,128]{2,1,0:T(8,128)(2,1)} %get-tuple-element.2101), channel_id=1, source_target_pairs={{24,0},{0,8},{8,16},{16,24},{25,1},{1,9},{9,17},{17,25},{26,2},{2,... | collective-permute-start | bytes 786440 | tf_op jit(solution)/shard_map/while/body/eval_jaxpr/ppermute | solution.py:27
  208.7 68.7 %copy-start.1 = (bf16[8192,128]{1,0:T(8,128)(2,1)S(1)}, bf16[8192,128]{1,0:T(8,128)(2,1)}, u32[]{:S(2)}) copy-start(bf16[8192,128]{1,0:T(8,128)(2,1)} %param.40) | copy-start | bytes 6291460
Sparse Core Ops, SparseCore 0:
  9.9 56.9 all-gather.1
  208.8 68.5 reduce-scatter.1
where the time goes:
time: 285 us; the launch traced here: 284 us
  waiting for transfers between devices  152 us (53%)
  matrix products  66.3 us (23%)
  other arithmetic  26.9 us (9%)
  local copies, waits for them, and re-layouts  15.8 us (6%)
  between operations  15.4 us (5%)
  loops' own time  6.3 us (2%)
    reduce_scatter x1, waiting for transfers between devices, shards(): lax.psum_scatter(partial_terms.astype(jnp.bfloat16), 'tp', scatter_dimens...  68.1 us
    all_gather x1, waiting for transfers between devices, shards(): gathered = lax.all_gather(checkpoint, 'tp', axis=1, tiled=True)  55.8 us
    ppermute x3, waiting for transfers between devices, from_behind(): return lax.ppermute(block, axis, route)  27.3 us
    dot_general x1, matrix products, shards(): jnp.dot(attended, output_weight, preferred_element_type=jnp.float32)  16.8 us
    dot_general x1, matrix products, shards(): jnp.dot(normed, query_weight, preferred_element_type=jnp.float32)  15.5 us
    dot_general x16, matrix products, absorb(): jnp.einsum('qhk,kd->qhd', weights.astype(jnp.bfloat16), value_rows, prefe...  14.3 us
    reduce_sum x16, other arithmetic, absorb(): new_total = totals[query_slot] * shrink + jnp.sum(weights, axis=-1)  8.28 us
    dot_general x16, matrix products, absorb(): jnp.einsum('qhd,kd->qhk', query_rows, key_rows, preferred_element_type=jn...  7.43 us
  transfers between devices with their start and end apart: 5, of which 5 were waited for; matrix products, arithmetic and copies ran while one was open for 1% of the time, Pallas kernels for 0%

commit v1 on v0

--- a/solution.py
+++ b/solution.py
@@ -55,7 +55,12 @@
     row_offsets = jnp.arange(block_rows, dtype=jnp.int32)
     own_blocks = lax.dynamic_slice_in_dim(block_order, 2 * context_rank, 2)
     own_positions = (own_blocks[:, None] * block_rows + row_offsets[None, :]).reshape(tok_rows)
-    gathered = lax.all_gather(checkpoint, "tp", axis=1, tiled=True)
+    ring = [checkpoint]
+    for hop in range(7):
+        ring.append(lax.ppermute(ring[-1], "tp", [(dev, (dev + 1) % 8) for dev in range(8)]))
+    gathered = jnp.roll(
+        jnp.concatenate(ring[::-1], axis=1), (lax.axis_index("tp") + 1) * ring[0].shape[1], axis=1
+    )
     widened = gathered.astype(jnp.float32)
     mean_square = jnp.mean(widened * widened, axis=-1, keepdims=True)
     normed = (widened * lax.rsqrt(mean_square + norm_epsilon) * norm_gain).astype(jnp.bfloat16)

time: 285 us -> 450 us (1.58)
  local copies, waits for them, and re-layouts: 15.8 us -> 66.4 us
  waiting for transfers between devices: 152 us -> 194 us
  other arithmetic: 26.9 us -> 64.9 us
  matrix products: 66.3 us -> 96.9 us
    ppermute x0 -> x7, waiting for transfers between devices: none -> 103 us  [shards(): lax.ppermute(ring[-1], 'tp', [(dev, (dev + 1) % 8) for dev in range(8)])]
    all_gather x1 -> x0, waiting for transfers between devices: 55.8 us -> none  [shards(): gathered = lax.all_gather(checkpoint, 'tp', axis=1, tiled=True)]
    dot_general x16, matrix products: 14.3 us -> 41.4 us  [absorb(): jnp.einsum('qhk,kd->qhd', weights.astype(jnp.bfloat16), value_rows, prefe...]
    scatter x16, other arithmetic: 0.19 us -> 21 us  [absorb(): totals.at[query_slot].set(new_total)]
    unnamed x12 -> x47, local copies, waits for them, and re-layouts: 1.54 us -> 20.3 us
    slice x8, local copies, waits for them, and re-layouts: 0.56 us -> 18.2 us  [absorb(): weighted[query_slot] * shrink[..., None]]
    mul x8, other arithmetic: 2.68 us -> 12.5 us  [absorb(): weighted[query_slot] * shrink[..., None]]
    dynamic_slice x8, local copies, waits for them, and re-layouts: 4.82 us -> 9.89 us  [one_block(): key_block = lax.dynamic_index_in_dim(block_order, stored, 0, keepdims=False)]
  transfers between devices with their start and end apart: 5 -> 11, of which waited for: 5 -> 11; matrix products, arithmetic and copies ran while one was open for 1% -> 1% of each run, Pallas kernels for 0% -> 0%
where the time goes in v1:
time: 450 us; the launch traced here: 447 us
  waiting for transfers between devices  194 us (43%)
  matrix products  96.9 us (22%)
  local copies, waits for them, and re-layouts  66.4 us (15%)
  other arithmetic  64.9 us (14%)
  between operations  15.7 us (3%)
  loops' own time  5.76 us (1%)
    ppermute x7, waiting for transfers between devices, shards(): lax.ppermute(ring[-1], 'tp', [(dev, (dev + 1) % 8) for dev in range(8)])  103 us
    reduce_scatter x1, waiting for transfers between devices, shards(): lax.psum_scatter(partial_terms.astype(jnp.bfloat16), 'tp', scatter_dimens...  67.5 us
    dot_general x16, matrix products, absorb(): jnp.einsum('qhk,kd->qhd', weights.astype(jnp.bfloat16), value_rows, prefe...  41.4 us
    ppermute x3, waiting for transfers between devices, from_behind(): return lax.ppermute(block, axis, route)  23.3 us
    scatter x16, other arithmetic, absorb(): totals.at[query_slot].set(new_total)  21 us
    unnamed x47, local copies, waits for them, and re-layouts  20.3 us
    slice x8, local copies, waits for them, and re-layouts, absorb(): weighted[query_slot] * shrink[..., None]  18.2 us
    dot_general x1, matrix products, shards(): jnp.dot(attended, output_weight, preferred_element_type=jnp.float32)  16.9 us
  transfers between devices with their start and end apart: 11, of which 11 were waited for; matrix products, arithmetic and copies ran while one was open for 1% of the time, Pallas kernels for 0%

profile of v1, /device:TPU:0, one launch (start us, length us, event | category | flops | bytes accessed | tf_op | source)
XLA Modules:
  0.0 446.9 jit_solution(7735541567533220449)
XLA Ops:
  7.8 15.6 %collective-permute-done.1 = bf16[512,1024]{1,0:T(8,128)(2,1)S(1)} collective-permute-done((bf16[512,1024]{1,0:T(8,128)(2,1)}, bf16[512,1024]{1,0:T(8,128)(2,1)S(1)}, u32[]{:S(2)}, u32[]{:S(2)}) %collective-permute-start.1) | collective-permute-done | bytes 1048608 | tf_op jit(solution)/shard_map/ppermute | solution.py:60
  23.3 15.1 %collective-permute-done.2 = bf16[512,1024]{1,0:T(8,128)(2,1)S(1)} collective-permute-done((bf16[512,1024]{1,0:T(8,128)(2,1)S(1)}, bf16[512,1024]{1,0:T(8,128)(2,1)S(1)}, u32[]{:S(2)}, u32[]{:S(2)}) %collective-permute-start.2) | collective-permute-done | bytes 1048608 | tf_op jit(solution)/shard_map/ppermute | solution.py:60
  39.5 15.1 %collective-permute-done.3 = bf16[512,1024]{1,0:T(8,128)(2,1)S(1)} collective-permute-done((bf16[512,1024]{1,0:T(8,128)(2,1)S(1)}, bf16[512,1024]{1,0:T(8,128)(2,1)S(1)}, u32[]{:S(2)}, u32[]{:S(2)}) %collective-permute-start.3) | collective-permute-done | bytes 1048608 | tf_op jit(solution)/shard_map/ppermute | solution.py:60
  55.6 15.1 %collective-permute-done.4 = bf16[512,1024]{1,0:T(8,128)(2,1)S(1)} collective-permute-done((bf16[512,1024]{1,0:T(8,128)(2,1)S(1)}, bf16[512,1024]{1,0:T(8,128)(2,1)S(1)}, u32[]{:S(2)}, u32[]{:S(2)}) %collective-permute-start.4) | collective-permute-done | bytes 1048608 | tf_op jit(solution)/shard_map/ppermute | solution.py:60
  71.7 15.1 %collective-permute-done.5 = bf16[512,1024]{1,0:T(8,128)(2,1)S(1)} collective-permute-done((bf16[512,1024]{1,0:T(8,128)(2,1)S(1)}, bf16[512,1024]{1,0:T(8,128)(2,1)S(1)}, u32[]{:S(2)}, u32[]{:S(2)}) %collective-permute-start.5) | collective-permute-done | bytes 1048608 | tf_op jit(solution)/shard_map/ppermute | solution.py:60
  87.8 15.2 %collective-permute-done.6 = bf16[512,1024]{1,0:T(8,128)(2,1)} collective-permute-done((bf16[512,1024]{1,0:T(8,128)(2,1)S(1)}, bf16[512,1024]{1,0:T(8,128)(2,1)}, u32[]{:S(2)}, u32[]{:S(2)}) %collective-permute-start.6) | collective-permute-done | bytes 1048608 | tf_op jit(solution)/shard_map/ppermute | solution.py:60
  106.3 12.2 %collective-permute-done.7 = bf16[512,1024]{1,0:T(8,128)(2,1)} collective-permute-done((bf16[512,1024]{1,0:T(8,128)(2,1)}, bf16[512,1024]{1,0:T(8,128)(2,1)}, u32[]{:S(2)}, u32[]{:S(2)}) %collective-permute-start.7) | collective-permute-done | bytes 1048608 | tf_op jit(solution)/shard_map/ppermute | solution.py:60
  127.4 5.7 %copy-done.5 = bf16[512,16384]{1,0:T(8,128)(2,1)} copy-done((bf16[512,16384]{1,0:T(8,128)(2,1)}, bf16[512,16384]{1,0:T(8,128)(2,1)S(1)}, u32[]{:S(2)}) %copy-start.5) | copy-done | bytes 16777240
  134.8 15.5 %fusion.106 = f32[512,1024]{0,1:T(8,128)} fusion(bf16[8192,1024]{1,0:T(8,128)(2,1)} %param.39, f32[8192]{0:T(1024)S(1)} %copy-done.17, f32[512]{0:T(512)S(1)} %add_rsqrt_fusion, bf16[512,16384]{1,0:T(8,128)(2,1)} %copy-done.5, s32[]{:T(128)S(6)} %select_n.187), kind=kOutput, calls=%fused_computation.181 | convolution fusion | flops 8606711808 | bytes 27297796 | tf_op jit(solution)/shard_map/dot_general | solution.py:67
  150.3 3.5 reshape_reshape.7
  153.8 4.4 subtract_convert_fusion
  158.2 2.2 pad_maximum_fusion
  160.4 2.1 copy.45
  162.5 1.9 copy.46
  164.5 6.0 %fusion.109 = f32[512,128]{0,1:T(8,128)S(1)} fusion(bf16[8192,128]{1,0:T(8,128)(2,1)S(1)} %copy-done, f32[8192]{0:T(1024)S(1)} %copy-done.17, f32[512]{0:T(512)S(1)} %add_rsqrt_fusion, bf16[512,16384]{1,0:T(8,128)(2,1)} %copy-done.5, s32[]{:T(128)S(6)} %select_n.187), kind=kOutput, calls=%fused_computation.182 | convolution fusion | flops 1090519040 | bytes 10782724 | tf_op jit(solution)/shard_map/dot_general | solution.py:68
  171.8 6.4 %fusion.95 = bf16[1,512,128]{2,1,0:T(8,128)(2,1)S(1)} fusion(bf16[8192,128]{1,0:T(8,128)(2,1)} %param.41, f32[8192]{0:T(1024)S(1)} %copy-done.17, f32[512]{0:T(512)S(1)} %add_rsqrt_fusion, bf16[512,16384]{1,0:T(8,128)(2,1)} %copy-done.5, s32[]{:T(128)S(6)} %select_n.187), kind=kOutput, calls=%fused_computation.140 | convolution fusion | flops 1090584576 | bytes 10651652 | tf_op jit(solution)/shard_map/dot_general | solution.py:69
  181.1 36.1 %while.100 = (s32[]{:T(128)}, f32[2,256,8]{1,2,0:T(8,128)S(1)}, f32[2,256,8]{1,2,0:T(8,128)}, f32[2,256,8,128]{3,1,2,0:T(8,128)}, s32[]{:T(128)}, /*index=5*/s32...) while((s32[]{:T(128)}, f32[2,256,8]{1,2,0:T(8,128)S(1)}, ...), condition=%wide.region_6.7_spmd.clone.clone, body=%wide.region_1.6_spmd.clone.clone.sunk | while | flops 551699200 | bytes 23058752 | solution.py:134
  184.5 2.3 slice.879
  186.7 3.1 fusion.153
  194.6 2.7 fusion.155
  202.5 2.3 slice.879
  204.8 3.1 fusion.153
  212.6 2.7 fusion.155
  217.2 134.3 %while.102 = (s32[]{:T(128)}, f32[2,256,8]{1,2,0:T(8,128)S(1)}, f32[2,256,8]{1,2,0:T(8,128)}, f32[2,256,8,128]{3,1,2,0:T(8,128)}, bf16[2,512,128]{2,1,0:T(8,128)...) while((s32[]{:T(128)}, f32[2,256,8]{1,2,0:T(8,128)S(1)}, ...), condition=%wide.region_14.15_spmd.clone.clone, body=%wide.region_7.0_spmd.clone.clone.sunk | while | flops 551699200 | bytes 24732756 | solution.py:150
  217.2 2.3 collective-permute-start
  219.5 6.6 %collective-permute-done = bf16[2,512,128]{2,1,0:T(8,128)(2,1)S(1)} collective-permute-done((bf16[2,512,128]{2,1,0:T(8,128)(2,1)}, bf16[2,512,128]{2,1,0:T(8,128)(2,1)S(1)}, u32[]{:S(2)}, u32[]{:S(2)}) %collective-permute-start) | collective-permute-done | bytes 262176 | tf_op jit(solution)/shard_map/while/body/eval_jaxpr/ppermute | solution.py:27
  226.6 35.0 %while.103 = (s32[]{:T(128)}, f32[2,256,8]{1,2,0:T(8,128)S(1)}, f32[2,256,8]{1,2,0:T(8,128)}, f32[2,256,8,128]{3,1,2,0:T(8,128)}, s32[]{:T(128)}, /*index=5*/s32...) while((s32[]{:T(128)}, f32[2,256,8]{1,2,0:T(8,128)S(1)}, ...), condition=%wide.region_13.13_spmd.clone, body=%wide.region_8.12_spmd.clone.sunk | while | flops 551699200 | bytes 23158172 | solution.py:134
  231.0 2.3 slice.889
  233.3 3.1 fusion.166
  248.5 2.3 slice.889
  250.8 3.1 fusion.166
  257.9 1.9 fusion.168
  262.3 8.4 %collective-permute-done = bf16[2,512,128]{2,1,0:T(8,128)(2,1)S(1)} collective-permute-done((bf16[2,512,128]{2,1,0:T(8,128)(2,1)}, bf16[2,512,128]{2,1,0:T(8,128)(2,1)S(1)}, u32[]{:S(2)}, u32[]{:S(2)}) %collective-permute-start) | collective-permute-done | bytes 262176 | tf_op jit(solution)/shard_map/while/body/eval_jaxpr/ppermute | solution.py:27
  271.2 35.0 %while.103 = (s32[]{:T(128)}, f32[2,256,8]{1,2,0:T(8,128)S(1)}, f32[2,256,8]{1,2,0:T(8,128)}, f32[2,256,8,128]{3,1,2,0:T(8,128)}, s32[]{:T(128)}, /*index=5*/s32...) while((s32[]{:T(128)}, f32[2,256,8]{1,2,0:T(8,128)S(1)}, ...), condition=%wide.region_13.13_spmd.clone, body=%wide.region_8.12_spmd.clone.sunk | while | flops 551699200 | bytes 23158172 | solution.py:134
  275.6 2.3 slice.889
  277.9 3.1 fusion.166
  293.1 2.3 slice.889
  295.3 3.1 fusion.166
  302.5 1.9 fusion.168
  306.9 8.4 %collective-permute-done = bf16[2,512,128]{2,1,0:T(8,128)(2,1)S(1)} collective-permute-done((bf16[2,512,128]{2,1,0:T(8,128)(2,1)}, bf16[2,512,128]{2,1,0:T(8,128)(2,1)S(1)}, u32[]{:S(2)}, u32[]{:S(2)}) %collective-permute-start) | collective-permute-done | bytes 262176 | tf_op jit(solution)/shard_map/while/body/eval_jaxpr/ppermute | solution.py:27
  315.8 35.0 %while.103 = (s32[]{:T(128)}, f32[2,256,8]{1,2,0:T(8,128)S(1)}, f32[2,256,8]{1,2,0:T(8,128)}, f32[2,256,8,128]{3,1,2,0:T(8,128)}, s32[]{:T(128)}, /*index=5*/s32...) while((s32[]{:T(128)}, f32[2,256,8]{1,2,0:T(8,128)S(1)}, ...), condition=%wide.region_13.13_spmd.clone, body=%wide.region_8.12_spmd.clone.sunk | while | flops 551699200 | bytes 23158172 | solution.py:134
  320.2 2.3 slice.889
  322.5 3.1 fusion.166
  337.7 2.3 slice.889
  339.9 3.1 fusion.166
  351.5 2.0 divide_convert_fusion
  354.1 16.9 %convolution_convert_fusion = bf16[512,8192]{1,0:T(8,128)(2,1)} fusion(bf16[1024,8192]{1,0:T(8,128)(2,1)} %param.42, bf16[64,8,8,128]{3,2,1,0:T(8,128)(2,1)S(1)} %bitcast.277), kind=kOutput, calls=%fused_computation.137 | convolution fusion | flops 8594128896 | bytes 26214400 | tf_op jit(solution)/shard_map/dot_general | solution.py:158
  372.5 67.5 %reduce-scatter.2.cloned.1.call-done = bf16[512,1024]{1,0:T(8,128)(2,1)} async-done(((bf16[512,8192]{1,0:T(8,128)(2,1)}), bf16[512,1024]{1,0:T(8,128)(2,1)}) %reduce-scatter.2.cloned.1.call-update) | async-done | bytes 1048592 | tf_op jit(solution)/shard_map/reduce_scatter | solution.py:159
  (221 shorter events, 110.2 us)
Async XLA Ops:
  7.2 157.3 %copy-start = (bf16[8192,128]{1,0:T(8,128)(2,1)S(1)}, bf16[8192,128]{1,0:T(8,128)(2,1)}, u32[]{:S(2)}) copy-start(bf16[8192,128]{1,0:T(8,128)(2,1)} %param.40) | copy-start | bytes 6291460
  7.2 432.8 %reduce-scatter.2.cloned.1.call-start = ((), (), s32[]{:S(2)}) async-start(), calls=%async_computation.1 | async-start | bytes 9437184 | tf_op jit(solution)/shard_map/reduce_scatter | solution.py:159
  7.2 16.1 %collective-permute-start.1 = (bf16[512,1024]{1,0:T(8,128)(2,1)}, bf16[512,1024]{1,0:T(8,128)(2,1)S(1)}, u32[]{:S(2)}, u32[]{:S(2)}) collective-permute-start(bf16[512,1024]{1,0:T(8,128)(2,1)} %param.37), channel_id=1, source_target_pairs={{0,1},{1,2},{2,3},{3,4},{4,5},{5,6},{6,7},{7,0},{8,9},{9,10},{10,1... | collective-permute-start | bytes 3145736 | tf_op jit(solution)/shard_map/ppermute | solution.py:60
  23.3 97.9 %copy-start.7 = (bf16[512,1024]{1,0:T(8,128)(2,1)}, bf16[512,1024]{1,0:T(8,128)(2,1)S(1)}, u32[]{:S(2)}) copy-start(bf16[512,1024]{1,0:T(8,128)(2,1)S(1)} %collective-permute-done.1) | copy-start | bytes 3145732
  23.3 15.1 %collective-permute-start.2 = (bf16[512,1024]{1,0:T(8,128)(2,1)S(1)}, bf16[512,1024]{1,0:T(8,128)(2,1)S(1)}, u32[]{:S(2)}, u32[]{:S(2)}) collective-permute-start(bf16[512,1024]{1,0:T(8,128)(2,1)S(1)} %collective-permute-done.1), channel_id=1, source_target_pairs={{0,1},{1,2},{2,3},{3,4},{4,5},{5,6},{6,7},{7,0},{8,9},{9,10},{10,1... | collective-permute-start | bytes 3145736 | tf_op jit(solution)/shard_map/ppermute | solution.py:60
  38.5 1.0 copy-start.9
  39.5 15.1 %collective-permute-start.3 = (bf16[512,1024]{1,0:T(8,128)(2,1)S(1)}, bf16[512,1024]{1,0:T(8,128)(2,1)S(1)}, u32[]{:S(2)}, u32[]{:S(2)}) collective-permute-start(bf16[512,1024]{1,0:T(8,128)(2,1)S(1)} %collective-permute-done.2), channel_id=1, source_target_pairs={{0,1},{1,2},{2,3},{3,4},{4,5},{5,6},{6,7},{7,0},{8,9},{9,10},{10,1... | collective-permute-start | bytes 3145736 | tf_op jit(solution)/shard_map/ppermute | solution.py:60
  54.6 1.0 copy-start.11
  55.6 15.1 %collective-permute-start.4 = (bf16[512,1024]{1,0:T(8,128)(2,1)S(1)}, bf16[512,1024]{1,0:T(8,128)(2,1)S(1)}, u32[]{:S(2)}, u32[]{:S(2)}) collective-permute-start(bf16[512,1024]{1,0:T(8,128)(2,1)S(1)} %collective-permute-done.3), channel_id=1, source_target_pairs={{0,1},{1,2},{2,3},{3,4},{4,5},{5,6},{6,7},{7,0},{8,9},{9,10},{10,1... | collective-permute-start | bytes 3145736 | tf_op jit(solution)/shard_map/ppermute | solution.py:60
  70.7 1.0 copy-start.13
  71.7 15.1 %collective-permute-start.5 = (bf16[512,1024]{1,0:T(8,128)(2,1)S(1)}, bf16[512,1024]{1,0:T(8,128)(2,1)S(1)}, u32[]{:S(2)}, u32[]{:S(2)}) collective-permute-start(bf16[512,1024]{1,0:T(8,128)(2,1)S(1)} %collective-permute-done.4), channel_id=1, source_target_pairs={{0,1},{1,2},{2,3},{3,4},{4,5},{5,6},{6,7},{7,0},{8,9},{9,10},{10,1... | collective-permute-start | bytes 3145736 | tf_op jit(solution)/shard_map/ppermute | solution.py:60
  86.8 1.0 copy-start.15
  87.8 15.2 %collective-permute-start.6 = (bf16[512,1024]{1,0:T(8,128)(2,1)S(1)}, bf16[512,1024]{1,0:T(8,128)(2,1)}, u32[]{:S(2)}, u32[]{:S(2)}) collective-permute-start(bf16[512,1024]{1,0:T(8,128)(2,1)S(1)} %collective-permute-done.5), channel_id=1, source_target_pairs={{0,1},{1,2},{2,3},{3,4},{4,5},{5,6},{6,7},{7,0},{8,9},{9,10},{10,1... | collective-permute-start | bytes 3145736 | tf_op jit(solution)/shard_map/ppermute | solution.py:60
  103.0 15.4 %collective-permute-start.7 = (bf16[512,1024]{1,0:T(8,128)(2,1)}, bf16[512,1024]{1,0:T(8,128)(2,1)}, u32[]{:S(2)}, u32[]{:S(2)}) collective-permute-start(bf16[512,1024]{1,0:T(8,128)(2,1)} %collective-permute-done.6), channel_id=1, source_target_pairs={{0,1},{1,2},{2,3},{3,4},{4,5},{5,6},{6,7},{7,0},{8,9},{9,10},{10,1... | collective-permute-start | bytes 3145736 | tf_op jit(solution)/shard_map/ppermute | solution.py:60
  106.3 14.9 %copy-start.16 = (bf16[512,1024]{1,0:T(8,128)(2,1)S(1)}, bf16[512,1024]{1,0:T(8,128)(2,1)}, u32[]{:S(2)}) copy-start(bf16[512,1024]{1,0:T(8,128)(2,1)} %copy-done.15) | copy-start | bytes 3145732
  119.8 1.5 copy-start.14
  121.2 1.3 copy-start.12
  121.3 1.4 copy-start.10
  122.5 1.3 copy-start.8
  122.8 1.3 copy-start.6
  127.4 5.7 %copy-start.5 = (bf16[512,16384]{1,0:T(8,128)(2,1)}, bf16[512,16384]{1,0:T(8,128)(2,1)S(1)}, u32[]{:S(2)}) copy-start(bf16[512,16384]{1,0:T(8,128)(2,1)S(1)} %constant_dynamic-update-slice_fusion) | copy-start | bytes 50331652
  133.1 1.7 copy-start.17
  217.2 8.9 %collective-permute-start = (bf16[2,512,128]{2,1,0:T(8,128)(2,1)}, bf16[2,512,128]{2,1,0:T(8,128)(2,1)S(1)}, u32[]{:S(2)}, u32[]{:S(2)}) collective-permute-start(bf16[2,512,128]{2,1,0:T(8,128)(2,1)} %get-tuple-element.2101), channel_id=1, source_target_pairs={{24,0},{0,8},{8,16},{16,24},{25,1},{1,9},{9,17},{17,25},{26,2},{2,... | collective-permute-start | bytes 786440 | tf_op jit(solution)/shard_map/while/body/eval_jaxpr/ppermute | solution.py:27
  229.8 0.6 copy-start.2
  233.3 3.1 copy-start.4
  236.4 0.7 copy-start.3
  247.3 0.6 copy-start.2
  250.8 3.1 copy-start.4
  253.9 0.7 copy-start.3
  262.3 8.4 %collective-permute-start = (bf16[2,512,128]{2,1,0:T(8,128)(2,1)}, bf16[2,512,128]{2,1,0:T(8,128)(2,1)S(1)}, u32[]{:S(2)}, u32[]{:S(2)}) collective-permute-start(bf16[2,512,128]{2,1,0:T(8,128)(2,1)} %get-tuple-element.2101), channel_id=1, source_target_pairs={{24,0},{0,8},{8,16},{16,24},{25,1},{1,9},{9,17},{17,25},{26,2},{2,... | collective-permute-start | bytes 786440 | tf_op jit(solution)/shard_map/while/body/eval_jaxpr/ppermute | solution.py:27
  274.4 0.6 copy-start.2
  277.9 3.1 copy-start.4
  281.0 0.7 copy-start.3
  291.9 0.6 copy-start.2
  295.3 3.1 copy-start.4
  298.4 0.7 copy-start.3
  306.9 8.4 %collective-permute-start = (bf16[2,512,128]{2,1,0:T(8,128)(2,1)}, bf16[2,512,128]{2,1,0:T(8,128)(2,1)S(1)}, u32[]{:S(2)}, u32[]{:S(2)}) collective-permute-start(bf16[2,512,128]{2,1,0:T(8,128)(2,1)} %get-tuple-element.2101), channel_id=1, source_target_pairs={{24,0},{0,8},{8,16},{16,24},{25,1},{1,9},{9,17},{17,25},{26,2},{2,... | collective-permute-start | bytes 786440 | tf_op jit(solution)/shard_map/while/body/eval_jaxpr/ppermute | solution.py:27
  319.0 0.6 copy-start.2
  322.5 3.1 copy-start.4
  325.6 0.7 copy-start.3
  336.5 0.6 copy-start.2
  339.9 3.1 copy-start.4
  343.0 0.7 copy-start.3
  371.0 69.0 %copy-start.1 = (bf16[8192,128]{1,0:T(8,128)(2,1)S(1)}, bf16[8192,128]{1,0:T(8,128)(2,1)}, u32[]{:S(2)}) copy-start(bf16[8192,128]{1,0:T(8,128)(2,1)} %param.40) | copy-start | bytes 6291460
Sparse Core Ops, SparseCore 0:
  371.1 68.8 reduce-scatter.1
